TPU v7x, 32 devices: a whole 2x2x4 slice. The times are simulated.
32 devices in a mesh: dp: 8 (over z, core), seq: 4 (over y, x).
Axes of the slice: x: 2, y: 2, z: 4, core: 2. Of those that a mesh axis runs over, the one named last changes fastest.
Arguments:
- tokens: bfloat16 [32, 256, 1024], P(('dp', 'seq')), may hold values from -6 to 6
- queries: bfloat16 [32, 256, 1024], P(('dp', 'seq')), may hold values from -240 to 240
- keys: bfloat16 [32, 256, 1024], P(('dp', 'seq')), may hold values from -7 to 7
- values: bfloat16 [32, 256, 1024], P(('dp', 'seq')), may hold values from -6 to 6
- ln_gain: bfloat16 [1024], replicated, may hold values from 0.5 to 1.5
- mean_in: bfloat16 [1024, 2048], P(None, 'seq'), may hold values from -0.1875 to 0.1875
- sigma_in: bfloat16 [1024, 2048], P(None, 'seq'), may hold values from 0.0039978027 to 0.029907227
- noise_in: bfloat16 [1024, 2048], P(None, 'seq'), may hold values from -4 to 4
- mean_out: bfloat16 [2048, 1024], P('seq'), may hold values from -0.125 to 0.125
- sigma_out: bfloat16 [2048, 1024], P('seq'), may hold values from 0.0019989014 to 0.014953613
- noise_out: bfloat16 [2048, 1024], P('seq'), may hold values from -4 to 4
- flip_in: int32 [32, 1024], P('dp'), may hold values from -1 to 1, as said below
- flip_mid: int32 [32, 2048], P('dp', 'seq'), may hold values from -1 to 1, as said below
- flip_hidden: int32 [32, 2048], P('dp', 'seq'), may hold values from -1 to 1, as said below
- flip_out: int32 [32, 1024], P('dp'), may hold values from -1 to 1, as said below
- cotangent: bfloat16 [32, 256, 1024], P(('dp', 'seq')), may hold values from -0.75 to 0.75
Outputs:
- block_out: bfloat16 [32, 256, 1024], P(('dp', 'seq'))
- resid_grad: bfloat16 [32, 256, 1024], P(('dp', 'seq'))
- grad_mean_in: float32 [1024, 2048], P(None, 'seq')
- grad_sigma_in: float32 [1024, 2048], P(None, 'seq')
- grad_mean_out: float32 [2048, 1024], P('seq')
- grad_sigma_out: float32 [2048, 1024], P('seq')
Inputs may be any that keep to these rules, and one draw needn't show every extreme that they name: `flip_in`: each entry is -1 or +1. `flip_mid`: each entry is -1 or +1. `flip_hidden`: each entry is -1 or +1. `flip_out`: each entry is -1 or +1.
All inputs are finite; a program needn't handle non-finite values.
Results may differ from a plain program's by a relative error of at most 0.018.
Values may be sent and summed in bfloat16 or wider, within the bound.
A program may use at most 128 MiB of HBM per device.

v0:
```python
import jax
import jax.numpy as jnp
from jax import lax
from jax.sharding import PartitionSpec as P

HEADS = 16


def gelu_slope(pre):
    cdf = 0.5 * (1.0 + lax.erf(pre * 0.7071067811865476))
    pdf = jnp.exp(-0.5 * pre * pre) * 0.3989422804014327
    return cdf + pre * pdf


def contract_first(left, right):
    return lax.dot_general(
        left, right, (((0,), (0,)), ((), ())), preferred_element_type=jnp.float32
    )


def contract_last(left, right):
    return lax.dot_general(
        left, right, (((1,), (1,)), ((), ())), preferred_element_type=jnp.float32
    )


def body(
    tokens,
    queries,
    keys,
    values,
    ln_gain,
    mean_in,
    sigma_in,
    noise_in,
    mean_out,
    sigma_out,
    noise_out,
    flip_in,
    flip_mid,
    flip_hidden,
    flip_out,
    cotangent,
):
    bf = jnp.bfloat16
    f32 = jnp.float32
    own_images, patches, width = tokens.shape
    hidden_local = mean_in.shape[1]
    head_dim = width // HEADS
    scale = head_dim ** (-0.5)
    pert_in = (sigma_in.astype(f32) * noise_in.astype(f32)).astype(bf)
    pert_out = (sigma_out.astype(f32) * noise_out.astype(f32)).astype(bf)
    query_heads = queries.reshape(own_images, patches, HEADS, head_dim)
    key_heads = keys.reshape(own_images, patches, HEADS, head_dim)
    value_heads = values.reshape(own_images, patches, HEADS, head_dim)
    scores = (
        jnp.einsum("bqhe,bkhe->bhqk", query_heads, key_heads, preferred_element_type=f32) * scale
    )
    top = jnp.max(scores, axis=-1, keepdims=True)
    expd = jnp.exp(scores - top)
    total = jnp.sum(expd, axis=-1)
    accum = jnp.einsum("bhqk,bkhe->bqhe", expd.astype(bf), value_heads, preferred_element_type=f32)
    attn_out = (
        (accum / jnp.transpose(total, (0, 2, 1))[..., None])
        .reshape(own_images, patches, width)
        .astype(bf)
    )
    resid = (tokens.astype(f32) + attn_out.astype(f32)).astype(bf)
    resid_f = resid.astype(f32)
    centered = resid_f - jnp.mean(resid_f, axis=-1, keepdims=True)
    rstd = lax.rsqrt(jnp.mean(centered * centered, axis=-1, keepdims=True) + 1e-06)
    ahat = centered * rstd
    gain_f = ln_gain.astype(f32)
    normed = (ahat * gain_f).astype(bf)
    in_signs = flip_in.astype(bf)[:, None, :]
    in_signs_f = flip_in.astype(f32)[:, None, :]
    mid_signs = flip_mid.astype(bf)[:, None, :]
    mid_signs_f = flip_mid.astype(f32)[:, None, :]
    hid_signs = flip_hidden.astype(bf)[:, None, :]
    hid_signs_f = flip_hidden.astype(f32)[:, None, :]
    out_signs = flip_out.astype(bf)[:, None, :]
    out_signs_f = flip_out.astype(f32)[:, None, :]
    gathered = lax.all_gather(normed, "seq", axis=0, tiled=True)
    count = gathered.shape[0]
    signs = in_signs
    flat = gathered.reshape(-1, width)
    flat_flip = (gathered * signs).reshape(-1, width)
    plain = jnp.dot(flat, mean_in, preferred_element_type=f32).reshape(count, patches, hidden_local)
    noisy = jnp.dot(flat_flip, pert_in, preferred_element_type=f32).reshape(
        count, patches, hidden_local
    )
    pre = plain + noisy * mid_signs_f
    group_images = pre.shape[0]
    rows = group_images * patches
    hidden = jax.nn.gelu(pre, approximate=False).astype(bf)
    flipped_hidden = hidden * hid_signs
    count = lax.axis_size("seq") * own_images
    hb = hidden.reshape(-1, hidden_local)
    hfb = flipped_hidden.reshape(-1, hidden_local)
    plain = jnp.dot(hb, mean_out, preferred_element_type=f32).reshape(count, patches, width)
    noisy = jnp.dot(hfb, pert_out, preferred_element_type=f32).reshape(count, patches, width)
    mixed = lax.psum_scatter(
        (plain + noisy * out_signs_f).astype(jnp.bfloat16), "seq", scatter_dimension=0, tiled=True
    ).astype(jnp.float32)
    block_out = (resid_f + mixed).astype(bf)
    cot_all = lax.all_gather(cotangent, "seq", axis=0, tiled=True)
    cot_flat = cot_all.reshape(rows, width)
    cot_flip_flat = (cot_all * out_signs).reshape(rows, width)
    dhidden = contract_last(cot_flat, mean_out).reshape(group_images, patches, hidden_local)
    dhidden = (
        dhidden
        + contract_last(cot_flip_flat, pert_out).reshape(group_images, patches, hidden_local)
        * hid_signs_f
    )
    dpre = (dhidden * gelu_slope(pre)).astype(bf)
    dpre_flip = dpre * mid_signs
    local_mean_out = contract_first(hidden.reshape(rows, hidden_local), cot_flat)
    local_sigma_out = contract_first(
        flipped_hidden.reshape(rows, hidden_local), cot_flip_flat
    ) * noise_out.astype(f32)
    grad_mean_out, grad_sigma_out = (
        lax.psum(local_mean_out.astype(jnp.bfloat16), "dp").astype(jnp.float32),
        lax.psum(local_sigma_out.astype(jnp.bfloat16), "dp").astype(jnp.float32),
    )
    local_mean_in = contract_first(gathered.reshape(rows, width), dpre.reshape(rows, hidden_local))
    local_flip_in = contract_first(
        (gathered * in_signs).reshape(rows, width), dpre_flip.reshape(rows, hidden_local)
    )
    local_sigma_in = local_flip_in * noise_in.astype(f32)
    count = lax.axis_size("seq") * own_images
    drows = dpre.reshape(-1, hidden_local)
    dflip_rows = dpre_flip.reshape(-1, hidden_local)
    signs = in_signs_f
    plain = contract_last(drows, mean_in).reshape(count, patches, width)
    noisy = contract_last(dflip_rows, pert_in).reshape(count, patches, width)
    dnormed = lax.psum_scatter(
        (plain + noisy * signs).astype(jnp.bfloat16), "seq", scatter_dimension=0, tiled=True
    ).astype(jnp.float32)
    grad_mean_in, grad_sigma_in = (
        lax.psum(local_mean_in.astype(jnp.bfloat16), "dp").astype(jnp.float32),
        lax.psum(local_sigma_in.astype(jnp.bfloat16), "dp").astype(jnp.float32),
    )
    scaled = dnormed * gain_f
    back = rstd * (
        scaled
        - jnp.mean(scaled, axis=-1, keepdims=True)
        - ahat * jnp.mean(scaled * ahat, axis=-1, keepdims=True)
    )
    resid_grad = (cotangent.astype(f32) + back).astype(bf)
    return (block_out, resid_grad, grad_mean_in, grad_sigma_in, grad_mean_out, grad_sigma_out)


def solution(mesh):
    return jax.shard_map(
        body,
        mesh=mesh,
        in_specs=(
            P(("dp", "seq"), None, None),
            P(("dp", "seq"), None, None),
            P(("dp", "seq"), None, None),
            P(("dp", "seq"), None, None),
            P(),
            P(None, "seq"),
            P(None, "seq"),
            P(None, "seq"),
            P("seq", None),
            P("seq", None),
            P("seq", None),
            P("dp", None),
            P("dp", "seq"),
            P("dp", "seq"),
            P("dp", None),
            P(("dp", "seq"), None, None),
        ),
        out_specs=(
            P(("dp", "seq"), None, None),
            P(("dp", "seq"), None, None),
            P(None, "seq"),
            P(None, "seq"),
            P("seq", None),
            P("seq", None),
        ),
        check_vma=False,
    )
```

profile of v0, /device:TPU:0, one launch (start us, length us, event | category | flops | bytes accessed | tf_op | source)
XLA Modules:
  0.0 289.0 jit_solution(1723222755347720097)
XLA Ops:
  13.9 1.5 convert_reduce_fusion
  18.0 37.0 %all-gather.3.cloned.1.call-done = bf16[4,256,1024]{2,1,0:T(8,128)(2,1)} async-done(((bf16[1,256,1024]{2,1,0:T(8,128)(2,1)}), bf16[4,256,1024]{2,1,0:T(8,128)(2,1)}) %all-gather.3.cloned.1.call-update) | async-done | bytes 2097168 | tf_op jit(solution)/shard_map/all_gather | solution.py:83
  55.0 3.3 %fusion.31 = f32[4,256,512]{2,1,0:T(8,128)S(1)} fusion(bf16[4,256,1024]{2,1,0:T(8,128)(2,1)} %all-gather.3.cloned.1.call-done, bf16[4,1024]{1,0:T(4,128)(2,1)S(1)} %get-tuple-element.19, bf16[1024,512]{1,0:T(8,128)(2,1)S(1)} %copy-done.7, bf16[1024,512]{1,0:T(8,128)(2,1)} %param.22), kind=kOutput, calls=%fused_computation.55 | convolution fusion | flops 1076887552 | bytes 6299648 | tf_op jit(solution)/shard_map/dot_general | solution.py:89
  58.3 1.9 fusion.77
  61.5 4.7 %fusion.8 = bf16[4,256,512]{2,1,0:T(8,128)(2,1)S(1)} fusion(f32[4,256,512]{2,1,0:T(8,128)S(1)} %get-tuple-element.28, u8[256,512]{1,0:T(8,128)(4,1)S(1)} %get-tuple-element.7, u8[256,512]{1,0:T(8,128)(4,1)S(1)} %get-tuple-element.6), kind=kLoop, calls=%fused_computation.18 | loop fusion | flops 36700160 | bytes 3407872 | tf_op jit(solution)/shard_map/convert_element_type | solution.py:95
  66.2 25.8 %all-gather.5.cloned.1.call-done = bf16[4,256,1024]{2,1,0:T(8,128)(2,1)} async-done(((bf16[1,256,1024]{2,1,0:T(8,128)(2,1)}), bf16[4,256,1024]{2,1,0:T(8,128)(2,1)}) %all-gather.5.cloned.1.call-update) | async-done | bytes 2097168 | tf_op jit(solution)/shard_map/all_gather | solution.py:106
  92.0 3.6 %fusion.27 = f32[4,256,512]{2,1,0:T(8,128)S(1)} fusion(bf16[4,256,1024]{2,1,0:T(8,128)(2,1)} %all-gather.5.cloned.1.call-done, bf16[4,1024]{1,0:T(4,128)(2,1)S(1)} %get-tuple-element.20, bf16[512,1024]{1,0:T(8,128)(2,1)} %param.26, bf16[512,1024]{1,0:T(8,128)(2,1)} %param.25), kind=kOutput, calls=%fused_computation.51 | convolution fusion | flops 1076887552 | bytes 6299648 | tf_op jit(solution)/shard_map/dot_general | solution.py:22
  95.8 2.0 fusion.14
  97.8 2.3 bitcast_convert_fusion.1
  100.1 2.3 fusion.3
  102.4 2.3 bitcast_convert_fusion
  104.6 2.4 fusion.5
  107.3 2.7 fusion.58
  110.0 2.6 add_convert_fusion
  112.7 2.6 fusion.56
  115.4 2.6 add_convert_fusion.1
  118.0 85.7 %all-reduce.5.cloned.1.call-done = (bf16[1024,512]{1,0:T(8,128)(2,1)}, bf16[1024,512]{1,0:T(8,128)(2,1)}, bf16[512,1024]{1,0:T(8,128)(2,1)}, bf16[512,1024]{1,0:T(8,128)(2,1)}) async-done(((bf16[1024,512]{1,0:T(8,128)(2,1)}, bf16[1024,512]{1,0:T(8,128)(2,1)}, bf16[512,1024]{1,0:T(8,128)(2,1)}, bf16[512,1024]{1,0:T(8,128)(2,1)}), (bf16[1024,512]{1,0:T(8,128)(2,1)}, bf16[1024,512]{1,0:T(8,128)(2,1)}, ...) | async-done | bytes 4194320 | tf_op jit(solution)/shard_map/psum | solution.py:140
  203.7 2.9 %convert_element_type.173 = f32[1024,512]{1,0:T(8,128)} convert(bf16[1024,512]{1,0:T(8,128)(2,1)} %get-tuple-element.10) | non-fusion elementwise | flops 524288 | bytes 3145728 | tf_op jit(solution)/shard_map/convert_element_type | solution.py:140
  206.7 1.6 convert_element_type.175
  208.3 1.6 convert_element_type.177
  209.8 1.6 convert_element_type.179
  211.4 30.4 %reduce-scatter.9.cloned.1.call-done = bf16[1,256,1024]{2,1,0:T(8,128)(2,1)} async-done(((bf16[4,256,1024]{2,1,0:T(8,128)(2,1)}), bf16[1,256,1024]{2,1,0:T(8,128)(2,1)}) %reduce-scatter.9.cloned.1.call-update) | async-done | bytes 524304
  243.2 36.6 %reduce-scatter.7.cloned.1.call-done = bf16[1,256,1024]{2,1,0:T(8,128)(2,1)} async-done(((bf16[4,256,1024]{2,1,0:T(8,128)(2,1)}), bf16[1,256,1024]{2,1,0:T(8,128)(2,1)}) %reduce-scatter.7.cloned.1.call-update) | async-done | bytes 524304
  279.8 2.6 fusion.50
  (83 shorter events, 12.3 us)
Async XLA Ops:
  7.2 51.1 %copy-start = (bf16[1024,512]{1,0:T(8,128)(2,1)S(1)}, bf16[1024,512]{1,0:T(8,128)(2,1)}, u32[]{:S(2)}) copy-start(bf16[1024,512]{1,0:T(8,128)(2,1)} %param.21) | copy-start | bytes 3145732
  7.2 2.7 copy-start.18
  7.2 47.8 %all-gather.3.cloned.1.call-start = ((), (), s32[]{:S(2)}) async-start(), calls=%async_computation.2 | async-start | bytes 2621440 | tf_op jit(solution)/shard_map/all_gather | solution.py:83
  13.9 4.0 %copy-start.22 = (s32[4,512]{1,0:T(4,128)S(1)}, s32[4,512]{1,0:T(4,128)}, u32[]{:S(2)}) copy-start(s32[4,512]{1,0:T(4,128)} %param.28) | copy-start | bytes 24580
  13.9 4.0 %copy-start.23 = (s32[4,512]{1,0:T(4,128)S(1)}, s32[4,512]{1,0:T(4,128)}, u32[]{:S(2)}) copy-start(s32[4,512]{1,0:T(4,128)} %param.29) | copy-start | bytes 24580
  13.9 4.0 %copy-start.20 = (s32[4,1024]{1,0:T(4,128)S(1)}, s32[4,1024]{1,0:T(4,128)}, u32[]{:S(2)}) copy-start(s32[4,1024]{1,0:T(4,128)} %param.27) | copy-start | bytes 49156
  13.9 4.0 %copy-start.21 = (s32[4,1024]{1,0:T(4,128)S(1)}, s32[4,1024]{1,0:T(4,128)}, u32[]{:S(2)}) copy-start(s32[4,1024]{1,0:T(4,128)} %param.30) | copy-start | bytes 49156
  13.9 41.0 %copy-start.7 = (bf16[1024,512]{1,0:T(8,128)(2,1)S(1)}, bf16[1024,512]{1,0:T(8,128)(2,1)}, u32[]{:S(2)}) copy-start(bf16[1024,512]{1,0:T(8,128)(2,1)} %param.23) | copy-start | bytes 3145732
  16.9 75.1 %all-gather.5.cloned.1.call-start = ((), (), s32[]{:S(2)}) async-start(), calls=%async_computation.3 | async-start | bytes 2621440 | tf_op jit(solution)/shard_map/all_gather | solution.py:106
  17.6 186.1 %all-reduce.5.cloned.1.call-start = ((), (), s32[]{:S(2)}) async-start(), calls=%async_computation.6 | async-start | bytes 8388608 | tf_op jit(solution)/shard_map/psum | solution.py:140
  55.0 3.3 %copy-start.25 = (bf16[4,256,1024]{2,1,0:T(8,128)(2,1)S(1)}, bf16[4,256,1024]{2,1,0:T(8,128)(2,1)}, u32[]{:S(2)}) copy-start(bf16[4,256,1024]{2,1,0:T(8,128)(2,1)} %all-gather.3.cloned.1.call-done) | copy-start | bytes 6291460
  92.0 3.6 %copy-start.3 = (bf16[4,256,1024]{2,1,0:T(8,128)(2,1)S(1)}, bf16[4,256,1024]{2,1,0:T(8,128)(2,1)}, u32[]{:S(2)}) copy-start(bf16[4,256,1024]{2,1,0:T(8,128)(2,1)} %all-gather.5.cloned.1.call-done) | copy-start | bytes 6291460
  92.0 3.6 %copy-start.5 = (f32[4,256,512]{2,1,0:T(8,128)S(1)}, f32[4,256,512]{2,1,0:T(8,128)}, u32[]{:S(2)}) copy-start(f32[4,256,512]{2,1,0:T(8,128)} %copy-done.4) | copy-start | bytes 6291460
  92.0 3.7 %copy-start.17 = (bf16[512,1024]{1,0:T(8,128)(2,1)S(1)}, bf16[512,1024]{1,0:T(8,128)(2,1)}, u32[]{:S(2)}) copy-start(bf16[512,1024]{1,0:T(8,128)(2,1)} %param.24) | copy-start | bytes 3145732
  97.8 2.3 copy-start.1
  107.0 134.8 %reduce-scatter.9.cloned.1.call-start = ((), (), s32[]{:S(2)}) async-start(), calls=%async_computation.5 | async-start | bytes 2621440
  107.3 2.7 copy-start.2
  107.3 2.7 copy-start.9
  107.3 2.7 copy-start.10
  112.7 167.2 %reduce-scatter.7.cloned.1.call-start = ((), (), s32[]{:S(2)}) async-start(), calls=%async_computation.4 | async-start | bytes 2621440
  112.7 2.7 copy-start.12
  112.7 2.7 copy-start.13
  203.7 2.9 %copy-start.16 = (bf16[1024,512]{1,0:T(8,128)(2,1)S(1)}, bf16[1024,512]{1,0:T(8,128)(2,1)}, u32[]{:S(2)}) copy-start(bf16[1024,512]{1,0:T(8,128)(2,1)} %get-tuple-element.11) | copy-start | bytes 3145732
  209.8 70.0 %copy-start.6 = (bf16[1,256,1024]{2,1,0:T(8,128)(2,1)S(1)}, bf16[1,256,1024]{2,1,0:T(8,128)(2,1)}, u32[]{:S(2)}) copy-start(bf16[1,256,1024]{2,1,0:T(8,128)(2,1)} %param.31) | copy-start | bytes 1572868
  (8 other events, 14.0 us)
Sparse Core Ops, SparseCore 0:
  17.0 37.8 all-gather.2
  56.8 35.1 all-gather.4
  107.1 96.5 all-reduce.4
  206.5 35.2 reduce-scatter.8
  244.6 35.1 reduce-scatter.6
where the time goes:
time: 289 us
  waiting for transfers between devices  216 us (75%)
  matrix products  32.2 us (11%)
  other arithmetic  20.2 us (7%)
  between operations  14.2 us (5%)
  local copies, waits for them, and re-layouts  5.66 us (2%)
    psum x1, waiting for transfers between devices, body(): lax.psum(local_mean_in.astype(jnp.bfloat16), 'dp').astype(jnp.float32)  85.7 us
    unnamed x7, waiting for transfers between devices  67.8 us
    all_gather x1, waiting for transfers between devices, body(): gathered = lax.all_gather(normed, 'seq', axis=0, tiled=True)  37 us
    all_gather x1, waiting for transfers between devices, body(): cot_all = lax.all_gather(cotangent, 'seq', axis=0, tiled=True)  25.8 us
    dot_general x4, matrix products, contract_last(): lax.dot_general(left, right, (((1,), (1,)), ((), ())), preferred_element_...  11 us
    dot_general x4, matrix products, contract_first(): lax.dot_general(left, right, (((0,), (0,)), ((), ())), preferred_element_...  9.14 us
  transfers between devices with their start and end apart: 5, of which 5 were waited for; matrix products, arithmetic and copies ran while one was open for 10% of the time, Pallas kernels for 0%

commit v1 on v0

--- a/solution.py
+++ b/solution.py
@@ -80,7 +80,12 @@
     hid_signs_f = flip_hidden.astype(f32)[:, None, :]
     out_signs = flip_out.astype(bf)[:, None, :]
     out_signs_f = flip_out.astype(f32)[:, None, :]
-    gathered = lax.all_gather(normed, "seq", axis=0, tiled=True)
+    ring = [normed]
+    for hop in range(3):
+        ring.append(lax.ppermute(ring[-1], "seq", [(dev, (dev + 1) % 4) for dev in range(4)]))
+    gathered = jnp.roll(
+        jnp.concatenate(ring[::-1], axis=0), (lax.axis_index("seq") + 1) * ring[0].shape[0], axis=0
+    )
     count = gathered.shape[0]
     signs = in_signs
     flat = gathered.reshape(-1, width)

time: 289 us -> 276 us (0.955)
  waiting for transfers between devices: 216 us -> 198 us
  starting transfers between devices: 0.6 us -> 5.92 us
    ppermute x0 -> x3, waiting for transfers between devices: none -> 42.5 us  [body(): lax.ppermute(ring[-1], 'seq', [(dev, (dev + 1) % 4) for dev in range(4)])]
    all_gather x1 -> x0, waiting for transfers between devices: 37 us -> none  [body(): gathered = lax.all_gather(normed, 'seq', axis=0, tiled=True)]
    all_gather x1, waiting for transfers between devices: 25.8 us -> 0.02 us  [body(): cot_all = lax.all_gather(cotangent, 'seq', axis=0, tiled=True)]
    ppermute x0 -> x3, starting transfers between devices: none -> 5.54 us  [body(): lax.ppermute(ring[-1], 'seq', [(dev, (dev + 1) % 4) for dev in range(4)])]
    unnamed x57 -> x65, local copies, waits for them, and re-layouts: 4.35 us -> 6.15 us
    unnamed x7 -> x6, waiting for transfers between devices: 67.8 us -> 67.3 us
  transfers between devices with their start and end apart: 5 -> 7, of which waited for: 5 -> 6; matrix products, arithmetic and copies ran while one was open for 10% -> 10% of each run, Pallas kernels for 0% -> 0%
where the time goes in v1:
time: 276 us
  waiting for transfers between devices  198 us (72%)
  matrix products  30.1 us (11%)
  other arithmetic  19.9 us (7%)
  between operations  14.2 us (5%)
  local copies, waits for them, and re-layouts  7.46 us (3%)
  starting transfers between devices  5.92 us (2%)
    psum x1, waiting for transfers between devices, body(): lax.psum(local_mean_in.astype(jnp.bfloat16), 'dp').astype(jnp.float32)  88.2 us
    unnamed x6, waiting for transfers between devices  67.3 us
    ppermute x3, waiting for transfers between devices, body(): lax.ppermute(ring[-1], 'seq', [(dev, (dev + 1) % 4) for dev in range(4)])  42.5 us
    dot_general x4, matrix products, contract_last(): lax.dot_general(left, right, (((1,), (1,)), ((), ())), preferred_element_...  11 us
    dot_general x4, matrix products, contract_first(): lax.dot_general(left, right, (((0,), (0,)), ((), ())), preferred_element_...  9.13 us
    unnamed x65, local copies, waits for them, and re-layouts  6.15 us
    ppermute x3, starting transfers between devices, body(): lax.ppermute(ring[-1], 'seq', [(dev, (dev + 1) % 4) for dev in range(4)])  5.54 us
  transfers between devices with their start and end apart: 7, of which 6 were waited for; matrix products, arithmetic and copies ran while one was open for 10% of the time, Pallas kernels for 0%

profile of v1, /device:TPU:0, one launch (start us, length us, event | category | flops | bytes accessed | tf_op | source)
XLA Modules:
  0.0 275.6 jit_solution(8147811761597464718)
XLA Ops:
  16.0 3.0 %collective-permute-start = (bf16[1,256,1024]{2,1,0:T(8,128)(2,1)S(1)}, bf16[1,256,1024]{2,1,0:T(8,128)(2,1)S(1)}, u32[]{:S(2)}, u32[]{:S(2)}) collective-permute-start(bf16[1,256,1024]{2,1,0:T(8,128)(2,1)S(1)} %fusion.49), channel_id=1, source_target_pairs={{0,1},{1,2},{2,3},{3,0},{4,5},{5,6},{6,7},{7,4},{8,9},{9,10},{10,1... | collective-permute-start | bytes 1572872 | tf_op jit(solution)/shard_map/ppermute | solution.py:85
  19.0 12.9 %collective-permute-done = bf16[1,256,1024]{2,1,0:T(8,128)(2,1)S(1)} collective-permute-done((bf16[1,256,1024]{2,1,0:T(8,128)(2,1)S(1)}, bf16[1,256,1024]{2,1,0:T(8,128)(2,1)S(1)}, u32[]{:S(2)}, u32[]{:S(2)}) %collective-permute-start) | collective-permute-done | bytes 524320 | tf_op jit(solution)/shard_map/ppermute | solution.py:85
  32.8 14.5 %collective-permute-done.1 = bf16[1,256,1024]{2,1,0:T(8,128)(2,1)S(1)} collective-permute-done((bf16[1,256,1024]{2,1,0:T(8,128)(2,1)S(1)}, bf16[1,256,1024]{2,1,0:T(8,128)(2,1)S(1)}, u32[]{:S(2)}, u32[]{:S(2)}) %collective-permute-start.1) | collective-permute-done | bytes 524320 | tf_op jit(solution)/shard_map/ppermute | solution.py:85
  47.3 1.7 collective-permute-start.2
  49.1 15.2 %collective-permute-done.2 = bf16[1,256,1024]{2,1,0:T(8,128)(2,1)S(1)} collective-permute-done((bf16[1,256,1024]{2,1,0:T(8,128)(2,1)S(1)}, bf16[1,256,1024]{2,1,0:T(8,128)(2,1)S(1)}, u32[]{:S(2)}, u32[]{:S(2)}) %collective-permute-start.2) | collective-permute-done | bytes 524320 | tf_op jit(solution)/shard_map/ppermute | solution.py:85
  67.9 1.9 fusion.81
  71.1 4.7 %fusion.8 = bf16[4,256,512]{2,1,0:T(8,128)(2,1)S(1)} fusion(f32[4,256,512]{2,1,0:T(8,128)S(1)} %get-tuple-element.28, u8[256,512]{1,0:T(8,128)(4,1)S(1)} %get-tuple-element.7, u8[256,512]{1,0:T(8,128)(4,1)S(1)} %get-tuple-element.6), kind=kLoop, calls=%fused_computation.18 | loop fusion | flops 36700160 | bytes 3407872 | tf_op jit(solution)/shard_map/convert_element_type | solution.py:100
  75.9 3.6 %fusion.27 = f32[4,256,512]{2,1,0:T(8,128)S(1)} fusion(bf16[4,256,1024]{2,1,0:T(8,128)(2,1)} %all-gather.2.cloned.1.call-done, bf16[4,1024]{1,0:T(4,128)(2,1)S(1)} %get-tuple-element.20, bf16[512,1024]{1,0:T(8,128)(2,1)} %param.26, bf16[512,1024]{1,0:T(8,128)(2,1)} %param.25), kind=kOutput, calls=%fused_computation.51 | convolution fusion | flops 1076887552 | bytes 6299648 | tf_op jit(solution)/shard_map/dot_general | solution.py:22
  79.6 2.0 fusion.14
  81.8 2.2 bitcast_convert_fusion.1
  84.1 2.3 fusion.3
  86.4 2.3 bitcast_convert_fusion
  88.6 2.3 fusion.5
  91.3 2.7 fusion.62
  94.0 2.6 add_convert_fusion
  96.7 2.6 fusion.60
  99.4 2.6 add_convert_fusion.1
  102.0 88.2 %all-reduce.5.cloned.1.call-done = (bf16[1024,512]{1,0:T(8,128)(2,1)}, bf16[1024,512]{1,0:T(8,128)(2,1)}, bf16[512,1024]{1,0:T(8,128)(2,1)}, bf16[512,1024]{1,0:T(8,128)(2,1)}) async-done(((bf16[1024,512]{1,0:T(8,128)(2,1)}, bf16[1024,512]{1,0:T(8,128)(2,1)}, bf16[512,1024]{1,0:T(8,128)(2,1)}, bf16[512,1024]{1,0:T(8,128)(2,1)}), (bf16[1024,512]{1,0:T(8,128)(2,1)}, bf16[1024,512]{1,0:T(8,128)(2,1)}, ...) | async-done | bytes 4194320 | tf_op jit(solution)/shard_map/psum | solution.py:145
  190.2 2.9 %convert_element_type.173 = f32[1024,512]{1,0:T(8,128)} convert(bf16[1024,512]{1,0:T(8,128)(2,1)} %get-tuple-element.10) | non-fusion elementwise | flops 524288 | bytes 3145728 | tf_op jit(solution)/shard_map/convert_element_type | solution.py:145
  193.1 1.6 convert_element_type.175
  194.8 1.6 convert_element_type.177
  197.9 30.6 %reduce-scatter.9.cloned.1.call-done = bf16[1,256,1024]{2,1,0:T(8,128)(2,1)} async-done(((bf16[4,256,1024]{2,1,0:T(8,128)(2,1)}), bf16[1,256,1024]{2,1,0:T(8,128)(2,1)}) %reduce-scatter.9.cloned.1.call-update) | async-done | bytes 524304
  229.9 36.6 %reduce-scatter.7.cloned.1.call-done = bf16[1,256,1024]{2,1,0:T(8,128)(2,1)} async-done(((bf16[4,256,1024]{2,1,0:T(8,128)(2,1)}), bf16[1,256,1024]{2,1,0:T(8,128)(2,1)}) %reduce-scatter.7.cloned.1.call-update) | async-done | bytes 524304
  266.5 2.6 fusion.54
  (96 shorter events, 18.1 us)
Async XLA Ops:
  7.2 60.7 %copy-start = (bf16[1024,512]{1,0:T(8,128)(2,1)S(1)}, bf16[1024,512]{1,0:T(8,128)(2,1)}, u32[]{:S(2)}) copy-start(bf16[1024,512]{1,0:T(8,128)(2,1)} %param.21) | copy-start | bytes 3145732
  7.2 2.7 copy-start.19
  7.2 68.7 %all-gather.2.cloned.1.call-start = ((), (), s32[]{:S(2)}) async-start(), calls=%async_computation.2 | async-start | bytes 2621440 | tf_op jit(solution)/shard_map/all_gather | solution.py:111
  13.9 18.9 %copy-start.25 = (s32[4,512]{1,0:T(4,128)S(1)}, s32[4,512]{1,0:T(4,128)}, u32[]{:S(2)}) copy-start(s32[4,512]{1,0:T(4,128)} %param.28) | copy-start | bytes 24580
  13.9 35.1 %copy-start.26 = (s32[4,512]{1,0:T(4,128)S(1)}, s32[4,512]{1,0:T(4,128)}, u32[]{:S(2)}) copy-start(s32[4,512]{1,0:T(4,128)} %param.29) | copy-start | bytes 24580
  13.9 35.1 %copy-start.23 = (s32[4,1024]{1,0:T(4,128)S(1)}, s32[4,1024]{1,0:T(4,128)}, u32[]{:S(2)}) copy-start(s32[4,1024]{1,0:T(4,128)} %param.27) | copy-start | bytes 49156
  13.9 35.1 %copy-start.24 = (s32[4,1024]{1,0:T(4,128)S(1)}, s32[4,1024]{1,0:T(4,128)}, u32[]{:S(2)}) copy-start(s32[4,1024]{1,0:T(4,128)} %param.30) | copy-start | bytes 49156
  16.0 15.9 %collective-permute-start = (bf16[1,256,1024]{2,1,0:T(8,128)(2,1)S(1)}, bf16[1,256,1024]{2,1,0:T(8,128)(2,1)S(1)}, u32[]{:S(2)}, u32[]{:S(2)}) collective-permute-start(bf16[1,256,1024]{2,1,0:T(8,128)(2,1)S(1)} %fusion.49), channel_id=1, source_target_pairs={{0,1},{1,2},{2,3},{3,0},{4,5},{5,6},{6,7},{7,4},{8,9},{9,10},{10,1... | collective-permute-start | bytes 1572872 | tf_op jit(solution)/shard_map/ppermute | solution.py:85
  31.9 15.4 %collective-permute-start.1 = (bf16[1,256,1024]{2,1,0:T(8,128)(2,1)S(1)}, bf16[1,256,1024]{2,1,0:T(8,128)(2,1)S(1)}, u32[]{:S(2)}, u32[]{:S(2)}) collective-permute-start(bf16[1,256,1024]{2,1,0:T(8,128)(2,1)S(1)} %collective-permute-done), channel_id=1, source_target_pairs={{0,1},{1,2},{2,3},{3,0},{4,5},{5,6},{6,7},{7,4},{8,9},{9,10},{10,1... | collective-permute-start | bytes 1572872 | tf_op jit(solution)/shard_map/ppermute | solution.py:85
  32.7 157.5 %all-reduce.5.cloned.1.call-start = ((), (), s32[]{:S(2)}) async-start(), calls=%async_computation.5 | async-start | bytes 8388608 | tf_op jit(solution)/shard_map/psum | solution.py:145
  47.3 16.9 %collective-permute-start.2 = (bf16[1,256,1024]{2,1,0:T(8,128)(2,1)S(1)}, bf16[1,256,1024]{2,1,0:T(8,128)(2,1)S(1)}, u32[]{:S(2)}, u32[]{:S(2)}) collective-permute-start(bf16[1,256,1024]{2,1,0:T(8,128)(2,1)S(1)} %collective-permute-done.1), channel_id=1, source_target_pairs={{0,1},{1,2},{2,3},{3,0},{4,5},{5,6},{6,7},{7,4},{8,9},{9,10},{10,1... | collective-permute-start | bytes 1572872 | tf_op jit(solution)/shard_map/ppermute | solution.py:85
  65.1 2.8 %copy-start.21 = (bf16[8,256,1024]{2,1,0:T(8,128)(2,1)}, bf16[8,256,1024]{2,1,0:T(8,128)(2,1)S(1)}, u32[]{:S(2)}) copy-start(bf16[8,256,1024]{2,1,0:T(8,128)(2,1)S(1)} %constant_dynamic-update-slice_fusion) | copy-start | bytes 12582916
  75.9 3.7 %copy-start.3 = (bf16[4,256,1024]{2,1,0:T(8,128)(2,1)S(1)}, bf16[4,256,1024]{2,1,0:T(8,128)(2,1)}, u32[]{:S(2)}) copy-start(bf16[4,256,1024]{2,1,0:T(8,128)(2,1)} %all-gather.2.cloned.1.call-done) | copy-start | bytes 6291460
  75.9 3.7 %copy-start.5 = (f32[4,256,512]{2,1,0:T(8,128)S(1)}, f32[4,256,512]{2,1,0:T(8,128)}, u32[]{:S(2)}) copy-start(f32[4,256,512]{2,1,0:T(8,128)} %copy-done.4) | copy-start | bytes 6291460
  75.9 3.7 %copy-start.18 = (bf16[512,1024]{1,0:T(8,128)(2,1)S(1)}, bf16[512,1024]{1,0:T(8,128)(2,1)}, u32[]{:S(2)}) copy-start(bf16[512,1024]{1,0:T(8,128)(2,1)} %param.24) | copy-start | bytes 3145732
  91.0 137.4 %reduce-scatter.9.cloned.1.call-start = ((), (), s32[]{:S(2)}) async-start(), calls=%async_computation.4 | async-start | bytes 2621440
  91.3 2.7 copy-start.2
  91.3 2.7 copy-start.9
  91.3 2.7 copy-start.11
  96.6 169.9 %reduce-scatter.7.cloned.1.call-start = ((), (), s32[]{:S(2)}) async-start(), calls=%async_computation.3 | async-start | bytes 2621440
  96.7 2.7 copy-start.13
  96.7 2.7 copy-start.14
  190.2 2.9 %copy-start.17 = (bf16[1024,512]{1,0:T(8,128)(2,1)S(1)}, bf16[1024,512]{1,0:T(8,128)(2,1)}, u32[]{:S(2)}) copy-start(bf16[1024,512]{1,0:T(8,128)(2,1)} %get-tuple-element.11) | copy-start | bytes 3145732
  196.3 70.2 %copy-start.6 = (bf16[1,256,1024]{2,1,0:T(8,128)(2,1)S(1)}, bf16[1,256,1024]{2,1,0:T(8,128)(2,1)}, u32[]{:S(2)}) copy-start(bf16[1,256,1024]{2,1,0:T(8,128)(2,1)} %param.31) | copy-start | bytes 1572868
  (11 other events, 19.5 us)
Sparse Core Ops, SparseCore 0:
  32.8 41.4 all-gather.1
  91.1 99.0 all-reduce.4
  193.2 35.2 reduce-scatter.8
  231.3 35.1 reduce-scatter.6
